TPU v7x, 256 devices: a whole 4x4x8 slice. The times are simulated.
256 devices in a mesh: rows: 32 (over z, y), chan: 8 (over x, core).
Axes of the slice: x: 4, y: 4, z: 8, core: 2. Of those that a mesh axis runs over, the one named last changes fastest.
Arguments:
- tokens: float32 [64, 768, 512], P('rows', 'chan'), may hold values from -6 to 6
- spectral: float32 [2, 64, 768, 128], P(None, None, 'chan'), may hold values from -6 to 6
- gain_in: float32 [2, 768], P(None, 'chan'), may hold values from 0.25 to 1.75
- gain_mid: float32 [2, 768], P(None, 'chan'), may hold values from 0.25 to 1.75
- expand: bfloat16 [2, 768, 3072], P(None, 'rows', 'chan'), may hold values from -0.21875 to 0.21875
- expand_bias: bfloat16 [2, 3072], P(None, 'chan'), may hold values from -3 to 3
- shrink: bfloat16 [2, 3072, 768], P(None, 'chan', 'rows'), may hold values from -0.21875 to 0.21875
Outputs:
- result: float32 [64, 768, 512], P('rows', 'chan')
All inputs are finite; a program needn't handle non-finite values.
Results may differ from a plain program's by a relative error of at most 0.017.
Values may be sent and summed in bfloat16 or wider, within the bound.
A program may use at most 64 MiB of HBM per device.

v0:
```python
import math
import jax
import jax.numpy as jnp
from jax import lax
from jax.sharding import Mesh
from jax.sharding import PartitionSpec as P

GRID = 64
CHAN = ("chan_0", "chan_1")


def from_everyone(value, axis):
    copies = jnp.broadcast_to(value, (lax.axis_size(axis), *value.shape))
    return lax.all_to_all(copies, axis, split_axis=0, concat_axis=0, tiled=True)


def taken_together(value, axis):
    return from_everyone(value, axis).sum(axis=0)


def in_one(arrays, axis):
    flat, at, finished = (jnp.concatenate([a.reshape(-1) for a in arrays]), 0, [])
    running = taken_together(flat, axis)
    for a in arrays:
        finished.append(running[at : at + a.size].reshape(a.shape))
        at += a.size
    return tuple(finished)


def sent_together(arrays, axis, split_dim, concat_dim, along):
    widths = [a.shape[along] for a in arrays]
    both = jnp.concatenate(arrays, axis=along)
    out = lax.all_to_all(both, axis, split_axis=split_dim, concat_axis=concat_dim, tiled=True)
    return tuple(jnp.split(out, [sum(widths[:k]) for k in range(1, len(widths))], axis=along))


def cut_rows(length, count):
    unit = 8 if length >= 8 * count else 1
    return [length // unit * k // count * unit for k in range(1, count)]


def stacked_from(value, axes, sequence):
    tiles = value[None]
    for k in sequence:
        tiles = lax.all_gather(tiles, axes[k], axis=0, tiled=True)
    held = [lax.axis_size(axes[k]) for k in reversed(sequence)]
    tiles = tiles.reshape(*held, *value.shape)
    turned = sorted(range(len(sequence)), key=lambda place: sequence[len(sequence) - 1 - place])
    return tiles.transpose(*turned, *range(len(sequence), tiles.ndim)).reshape(-1, *value.shape)


def in_order(tiles, dim):
    dims = list(tiles.shape[1:])
    dims[dim] *= tiles.shape[0]
    return jnp.moveaxis(tiles, 0, dim).reshape(dims)


def spread_gather(value, axes, dim):
    widest = max(range(max(1, value.ndim - 1)), key=lambda d: value.shape[d])
    count, finished = (len(axes), [])
    for leading, share in enumerate(
        jnp.split(value, cut_rows(value.shape[widest], count), axis=widest)
    ):
        if share.size:
            sequence = [(leading - k) % count for k in range(count)]
            finished.append(stacked_from(share, axes, sequence))
    return in_order(jnp.concatenate(finished, axis=widest + 1), dim)


def gather_directly(value, axis, dim):
    return in_order(from_everyone(value, axis), dim)


def in_blocks(value, dim, peers):
    before, after = (value.shape[:dim], value.shape[dim + 1 :])
    return jnp.moveaxis(value.reshape(*before, peers, -1, *after), dim, 0)


def summed_on_arrival(value, axis, dim):
    tiles = in_blocks(value, dim, lax.axis_size(axis))
    arrived = lax.all_to_all(tiles, axis, split_axis=0, concat_axis=0, tiled=True)
    return arrived.astype(jnp.float32).sum(axis=0)


def tables(count):
    index = jnp.arange(count, dtype=jnp.int32)
    product = index[:, None] * index[None, :] % count
    angle = product.astype(jnp.float32) * (2.0 * math.pi / count)
    return (jnp.cos(angle), jnp.sin(angle))


def finish_norm(values, sums, squares, total, gain):
    mean = sums / total
    var = squares / total - mean * mean
    return (values - mean[:, None, :]) * lax.rsqrt(var + 1e-06)[:, None, :] * gain[None, :, None]


def reflect(values):
    return jnp.roll(jnp.flip(values, -1), 1, -1)


def row_transform(a_re, a_im, cosine, sine, highest):
    b_re = jnp.einsum("hcbk,hj->cbkj", a_re, cosine, precision=highest) + jnp.einsum(
        "hcbk,hj->cbkj", a_im, sine, precision=highest
    )
    b_im = jnp.einsum("hcbk,hj->cbkj", a_im, cosine, precision=highest) - jnp.einsum(
        "hcbk,hj->cbkj", a_re, sine, precision=highest
    )
    return (b_re, b_im)


def row_inverse(c_re, c_im, cosine, sine, highest):
    d_re = jnp.einsum("cbkj,jh->hcbk", c_re, cosine, precision=highest) - jnp.einsum(
        "cbkj,jh->hcbk", c_im, sine, precision=highest
    )
    d_im = jnp.einsum("cbkj,jh->hcbk", c_im, cosine, precision=highest) + jnp.einsum(
        "cbkj,jh->hcbk", c_re, sine, precision=highest
    )
    return (d_re, d_im)


def per_device(tokens, spectral, gain_in, gain_mid, expand, expand_bias, shrink):
    highest = lax.Precision.HIGHEST
    local_rows, local_chan, merged = tokens.shape
    channels = local_chan * lax.axis_size(CHAN)
    images = merged // GRID
    cosine, sine = tables(GRID)
    half = GRID // 2
    parity = jnp.where(jnp.arange(GRID, dtype=jnp.int32) % 2 == 0, 1.0, -1.0).astype(jnp.float32)
    state = tokens
    for layer in range(expand.shape[0]):
        sums = in_one((jnp.sum(state, axis=1), jnp.sum(state * state, axis=1)), CHAN)
        normed = finish_norm(state, sums[0], sums[1], channels, gain_in[layer]).reshape(
            local_rows, local_chan, images, GRID
        )
        spec_layer = spectral[layer]
        cos_half = cosine[:, :half]
        sin_half = (-sine[:, :half]).at[:, 0].set(parity)
        a_re = jnp.einsum("hcbw,wk->hcbk", normed, cos_half, precision=highest)
        a_im = jnp.einsum("hcbw,wk->hcbk", normed, sin_half, precision=highest)
        a_re, a_im = tuple(
            (
                part.astype(jnp.float32)
                for part in sent_together(
                    (a_re.astype(jnp.bfloat16), a_im.astype(jnp.bfloat16)), "rows", 3, 0, 1
                )
            )
        )
        b_re, b_im = row_transform(a_re, a_im, cosine, sine, highest)
        owned = a_re.shape[3]
        column = lax.axis_index("rows") * owned + jnp.arange(owned, dtype=jnp.int32)
        mine = jnp.take(spec_layer, column, axis=0)
        mirror = jnp.take(spec_layer, (GRID - column) % GRID, axis=0)
        g_re = (mine[:, :, :GRID] + reflect(mirror[:, :, :GRID])).transpose(1, 0, 2)[:, None]
        g_im = (mine[:, :, GRID:] - reflect(mirror[:, :, GRID:])).transpose(1, 0, 2)[:, None]
        gen_re = b_re * g_re - b_im * g_im
        gen_im = b_re * g_im + b_im * g_re
        first = spec_layer[0]
        middle_col = spec_layer[half]
        low_re = 0.5 * (first[:, :GRID] + reflect(first[:, :GRID]))
        low_im = 0.5 * (first[:, GRID:] - reflect(first[:, GRID:]))
        top_re = 0.5 * (middle_col[:, :GRID] + reflect(middle_col[:, :GRID]))
        top_im = 0.5 * (middle_col[:, GRID:] - reflect(middle_col[:, GRID:]))
        plus_re = (0.5 * (low_re + top_re))[:, None, None, :]
        plus_im = (0.5 * (low_im + top_im))[:, None, None, :]
        minus_re = (0.5 * (low_re - top_re))[:, None, None, :]
        minus_im = (0.5 * (low_im - top_im))[:, None, None, :]
        back_re = reflect(b_re)
        back_im = -reflect(b_im)
        zero_re = b_re * plus_re - b_im * plus_im + back_re * minus_re - back_im * minus_im
        zero_im = b_re * plus_im + b_im * plus_re + back_re * minus_im + back_im * minus_re
        is_zero = (column == 0)[None, None, :, None]
        c_re = jnp.where(is_zero, zero_re, gen_re)
        c_im = jnp.where(is_zero, zero_im, gen_im)
        d_re, d_im = row_inverse(c_re, c_im, cosine, sine, highest)
        d_re, d_im = tuple(
            (
                part.astype(jnp.float32)
                for part in sent_together(
                    (d_re.astype(jnp.bfloat16), d_im.astype(jnp.bfloat16)), "rows", 0, 3, 1
                )
            )
        )
        last_sin = sine[:half, :].at[0, :].set(-parity)
        mixed = (
            jnp.einsum("hcbk,kw->hcbw", d_re, cosine[:half, :], precision=highest)
            - jnp.einsum("hcbk,kw->hcbw", d_im, last_sin, precision=highest)
        ) * (1.0 / (GRID * GRID))
        mixed = mixed.reshape(local_rows, local_chan, merged)
        middle = in_one((jnp.sum(mixed, axis=1), jnp.sum(mixed * mixed, axis=1)), CHAN)
        normed2 = finish_norm(mixed, middle[0], middle[1], channels, gain_mid[layer]).astype(
            jnp.bfloat16
        )
        flat = normed2.transpose(0, 2, 1).reshape(-1, local_chan)
        whole = spread_gather(flat, CHAN, 1)
        pre = jnp.dot(
            whole, gather_directly(expand[layer], "rows", 0), preferred_element_type=jnp.float32
        )
        hidden = jax.nn.gelu(pre + expand_bias[layer].astype(jnp.float32), approximate=True).astype(
            jnp.bfloat16
        )
        terms = jnp.dot(
            hidden, gather_directly(shrink[layer], "rows", 1), preferred_element_type=jnp.float32
        )
        branch = summed_on_arrival(terms.astype(jnp.bfloat16), CHAN, 1).astype(jnp.bfloat16)
        update = (
            branch.astype(jnp.float32).reshape(local_rows, merged, local_chan).transpose(0, 2, 1)
        )
        state = state + update
    return state


def solution(mesh):
    torus = Mesh(mesh.devices.reshape(mesh.shape["rows"], 4, 2), ("rows", "chan_0", "chan_1"))
    placed = (
        P("rows", CHAN, None),
        P(None, None, CHAN, None),
        P(None, CHAN),
        P(None, CHAN),
        P(None, "rows", CHAN),
        P(None, CHAN),
        P(None, CHAN, "rows"),
    )
    return jax.shard_map(
        per_device, mesh=torus, in_specs=placed, out_specs=P("rows", CHAN, None), check_vma=False
    )
```

profile of v0, /device:TPU:1, one launch (start us, length us, event | category | flops | bytes accessed | tf_op | source)
XLA Modules:
  0.0 321.1 jit_solution(17089204497144788136)
XLA Ops:
  1.8 6.5 %all-to-all-start = ((f32[8,1,2048]{2,1,0:T(1,128)}), f32[8,1,2048]{2,1,0:T(1,128)S(1)}, u32[]{:S(2)}, u32[]{:S(2)}) async-start(f32[8,1,2048]{2,1,0:T(1,128)} %broadcast_in_dim.92), calls=%async_computation | async-start | bytes 131072 | tf_op jit(solution)/shard_map/all_to_all | solution.py:14
  17.7 10.5 %all-to-all-start.1 = ((bf16[2,192,8,32]{1,2,0,3:T(8,128)(2,1)}), bf16[2,192,8,32]{1,2,0,3:T(8,128)(2,1)S(1)}, u32[]{:S(2)}, u32[]{:S(2)}) async-start(bf16[2,192,8,32]{1,2,0,3:T(8,128)(2,1)} %copy.230), calls=%async_computation.1 | async-start | bytes 524288 | tf_op jit(solution)/shard_map/all_to_all | solution.py:33
  29.0 11.2 %all-to-all-done.1 = bf16[2,192,8,32]{1,2,0,3:T(8,128)(2,1)S(1)} async-done(((bf16[2,192,8,32]{1,2,0,3:T(8,128)(2,1)}), bf16[2,192,8,32]{1,2,0,3:T(8,128)(2,1)S(1)}, u32[]{:S(2)}, u32[]{:S(2)}) %all-to-all-start.1) | async-done | bytes 196640 | tf_op jit(solution)/shard_map/all_to_all | solution.py:33
  50.1 10.2 %all-to-all-done.2 = bf16[64,192,8,1]{1,2,3,0:T(8,128)(2,1)S(1)} async-done(((bf16[64,192,8,1]{1,2,3,0:T(8,128)(2,1)}), bf16[64,192,8,1]{1,2,3,0:T(8,128)(2,1)S(1)}, u32[]{:S(2)}, u32[]{:S(2)}) %all-to-all-start.2) | async-done | bytes 196640 | tf_op jit(solution)/shard_map/all_to_all | solution.py:33
  62.3 7.9 %all-to-all-start.3 = ((f32[8,1,2048]{2,1,0:T(1,128)}), f32[8,1,2048]{2,1,0:T(1,128)S(1)}, u32[]{:S(2)}, u32[]{:S(2)}) async-start(f32[8,1,2048]{2,1,0:T(1,128)} %broadcast_in_dim.97), calls=%async_computation.3 | async-start | bytes 131072 | tf_op jit(solution)/shard_map/all_to_all | solution.py:14
  70.2 4.8 %all-to-all-done.3 = f32[8,1,2048]{2,1,0:T(1,128)S(1)} async-done(((f32[8,1,2048]{2,1,0:T(1,128)}), f32[8,1,2048]{2,1,0:T(1,128)S(1)}, u32[]{:S(2)}, u32[]{:S(2)}) %all-to-all-start.3) | async-done | bytes 65568 | tf_op jit(solution)/shard_map/all_to_all | solution.py:14
  80.2 17.2 %all-to-all-done.4 = bf16[32,24,384]{2,1,0:T(8,128)(2,1)S(1)} async-done(((bf16[32,24,384]{2,1,0:T(8,128)(2,1)}), bf16[32,24,384]{2,1,0:T(8,128)(2,1)S(1)}, u32[]{:S(2)}, u32[]{:S(2)}) %all-to-all-start.4) | async-done | bytes 589856 | tf_op jit(solution)/shard_map/all_to_all | solution.py:14
  98.3 5.2 %all-to-all-start.5 = ((bf16[32,384,24]{1,2,0:T(8,128)(2,1)}), bf16[32,384,24]{1,2,0:T(8,128)(2,1)S(1)}, u32[]{:S(2)}, u32[]{:S(2)}) async-start(bf16[32,384,24]{1,2,0:T(8,128)(2,1)} %broadcast_in_dim.99), calls=%async_computation.5 | async-start | bytes 1179648 | tf_op jit(solution)/shard_map/all_to_all | solution.py:14
  103.6 10.5 %all_gather.24 = bf16[4,512,96]{1,2,0:T(8,128)(2,1)S(1)} all-gather(bf16[1,512,96]{1,2,0:T(8,128)(2,1)S(1)} %get-tuple-element.96), channel_id=1, replica_groups=mesh['rows'=32,'chan_0'=4,'chan_1'=2] {'chan_0'}, dimensions={0}, use_global_device_ids=true | all-gather | bytes 491520 | tf_op jit(solution)/shard_map/all_gather | solution.py:45
  114.2 6.0 %all_gather.25 = bf16[8,512,96]{1,2,0:T(8,128)(2,1)S(1)} all-gather(bf16[4,512,96]{1,2,0:T(8,128)(2,1)S(1)} %all_gather.24), channel_id=1, replica_groups=mesh['rows'=32,'chan_0'=4,'chan_1'=2] {'chan_1'}, dimensions={0}, use_global_device_ids=true | all-gather | bytes 1179648 | tf_op jit(solution)/shard_map/all_gather | solution.py:45
  122.2 11.1 %all_gather.27 = bf16[8,512,96]{1,2,0:T(8,128)(2,1)S(1)} all-gather(bf16[2,512,96]{1,2,0:T(8,128)(2,1)S(1)} %all_gather.26), channel_id=1, replica_groups=mesh['rows'=32,'chan_0'=4,'chan_1'=2] {'chan_0'}, dimensions={0}, use_global_device_ids=true | all-gather | bytes 983040 | tf_op jit(solution)/shard_map/all_gather | solution.py:45
  136.7 7.0 %all-to-all-start.6 = ((bf16[8,1024,96]{1,2,0:T(8,128)(2,1)}), bf16[8,1024,96]{1,2,0:T(8,128)(2,1)S(1)}, u32[]{:S(2)}, u32[]{:S(2)}) async-start(bf16[8,1024,96]{1,2,0:T(8,128)(2,1)} %bitcast.279), calls=%async_computation.6 | async-start | bytes 3145728 | tf_op jit(solution)/shard_map/all_to_all | solution.py:81
  144.3 20.1 %all-to-all-done.6 = bf16[8,1024,96]{1,2,0:T(8,128)(2,1)S(1)} async-done(((bf16[8,1024,96]{1,2,0:T(8,128)(2,1)}), bf16[8,1024,96]{1,2,0:T(8,128)(2,1)S(1)}, u32[]{:S(2)}, u32[]{:S(2)}) %all-to-all-start.6) | async-done | bytes 1572896 | tf_op jit(solution)/shard_map/all_to_all | solution.py:81
  170.1 4.4 %all-to-all-done.7 = f32[8,1,2048]{2,1,0:T(1,128)S(1)} async-done(((f32[8,1,2048]{2,1,0:T(1,128)}), f32[8,1,2048]{2,1,0:T(1,128)S(1)}, u32[]{:S(2)}, u32[]{:S(2)}) %all-to-all-start.7) | async-done | bytes 65568 | tf_op jit(solution)/shard_map/all_to_all | solution.py:14
  176.9 9.4 %all-to-all-start.8 = ((bf16[2,192,8,32]{1,2,0,3:T(8,128)(2,1)}), bf16[2,192,8,32]{1,2,0,3:T(8,128)(2,1)S(1)}, u32[]{:S(2)}, u32[]{:S(2)}) async-start(bf16[2,192,8,32]{1,2,0,3:T(8,128)(2,1)} %copy.251), calls=%async_computation.8 | async-start | bytes 524288 | tf_op jit(solution)/shard_map/all_to_all | solution.py:33
  187.0 10.6 %all-to-all-done.8 = bf16[2,192,8,32]{1,2,0,3:T(8,128)(2,1)S(1)} async-done(((bf16[2,192,8,32]{1,2,0,3:T(8,128)(2,1)}), bf16[2,192,8,32]{1,2,0,3:T(8,128)(2,1)S(1)}, u32[]{:S(2)}, u32[]{:S(2)}) %all-to-all-start.8) | async-done | bytes 196640 | tf_op jit(solution)/shard_map/all_to_all | solution.py:33
  202.2 14.9 %all_to_all.126 = bf16[64,192,8,1]{1,2,3,0:T(8,128)(2,1)S(1)} all-to-all(bf16[64,192,8,1]{1,2,3,0:T(8,128)(2,1)S(1)} %copy.262), channel_id=1, replica_groups=mesh['rows'=32,'chan_0'=4,'chan_1'=2] {'rows'}, dimensions={0} | all-to-all | bytes 393216 | tf_op jit(solution)/shard_map/all_to_all | solution.py:33
  218.5 11.0 %all_to_all.127 = f32[8,1,2048]{2,1,0:T(1,128)S(1)} all-to-all(f32[8,1,2048]{2,1,0:T(1,128)S(1)} %broadcast_in_dim.101), channel_id=1, replica_groups=mesh['rows'=32,'chan_0'=4,'chan_1'=2] {'chan_0','chan_1'}, dimensions={0} | all-to-all | bytes 131072 | tf_op jit(solution)/shard_map/all_to_all | solution.py:14
  234.5 17.3 %all-to-all-done.11 = bf16[32,24,384]{2,1,0:T(8,128)(2,1)S(1)} async-done(((bf16[32,24,384]{2,1,0:T(8,128)(2,1)}), bf16[32,24,384]{2,1,0:T(8,128)(2,1)S(1)}, u32[]{:S(2)}, u32[]{:S(2)}) %all-to-all-start.11) | async-done | bytes 589856 | tf_op jit(solution)/shard_map/all_to_all | solution.py:14
  252.7 5.3 %all-to-all-start.12 = ((bf16[32,384,24]{1,2,0:T(8,128)(2,1)}), bf16[32,384,24]{1,2,0:T(8,128)(2,1)}, u32[]{:S(2)}, u32[]{:S(2)}) async-start(bf16[32,384,24]{1,2,0:T(8,128)(2,1)} %broadcast_in_dim.103), calls=%async_computation.12 | async-start | bytes 1179648 | tf_op jit(solution)/shard_map/all_to_all | solution.py:14
  258.2 10.8 %all_gather.28 = bf16[4,512,96]{1,2,0:T(8,128)(2,1)S(1)} all-gather(bf16[1,512,96]{1,2,0:T(8,128)(2,1)S(1)} %get-tuple-element.94), channel_id=1, replica_groups=mesh['rows'=32,'chan_0'=4,'chan_1'=2] {'chan_0'}, dimensions={0}, use_global_device_ids=true | all-gather | bytes 491520 | tf_op jit(solution)/shard_map/all_gather | solution.py:45
  269.0 5.9 %all_gather.29 = bf16[8,512,96]{1,2,0:T(8,128)(2,1)S(1)} all-gather(bf16[4,512,96]{1,2,0:T(8,128)(2,1)S(1)} %all_gather.28), channel_id=1, replica_groups=mesh['rows'=32,'chan_0'=4,'chan_1'=2] {'chan_1'}, dimensions={0}, use_global_device_ids=true | all-gather | bytes 1179648 | tf_op jit(solution)/shard_map/all_gather | solution.py:45
  277.0 10.9 %all_gather.31 = bf16[8,512,96]{1,2,0:T(8,128)(2,1)S(1)} all-gather(bf16[2,512,96]{1,2,0:T(8,128)(2,1)S(1)} %all_gather.30), channel_id=1, replica_groups=mesh['rows'=32,'chan_0'=4,'chan_1'=2] {'chan_0'}, dimensions={0}, use_global_device_ids=true | all-gather | bytes 983040 | tf_op jit(solution)/shard_map/all_gather | solution.py:45
  292.3 27.6 %all_to_all.128 = bf16[8,1024,96]{1,2,0:T(8,128)(2,1)S(1)} all-to-all(bf16[8,1024,96]{1,2,0:T(8,128)(2,1)} %bitcast.282), channel_id=1, replica_groups=mesh['rows'=32,'chan_0'=4,'chan_1'=2] {'chan_0','chan_1'}, dimensions={0} | all-to-all | bytes 3145728 | tf_op jit(solution)/shard_map/all_to_all | solution.py:81
  (187 shorter events, 63.5 us)
Async XLA Ops:
  1.8 13.6 %all-to-all-start = ((f32[8,1,2048]{2,1,0:T(1,128)}), f32[8,1,2048]{2,1,0:T(1,128)S(1)}, u32[]{:S(2)}, u32[]{:S(2)}) async-start(f32[8,1,2048]{2,1,0:T(1,128)} %broadcast_in_dim.92), calls=%async_computation | async-start | bytes 131072 | tf_op jit(solution)/shard_map/all_to_all | solution.py:14
  8.2 3.6 %copy-start = (f32[2,96,512]{2,1,0:T(8,128)S(1)}, f32[2,96,512]{2,1,0:T(8,128)}, u32[]{:S(2)}) copy-start(f32[2,96,512]{2,1,0:T(8,128)} %param.17) | copy-start | bytes 1179652
  11.7 2.7 copy-start.4
  17.7 22.5 %all-to-all-start.1 = ((bf16[2,192,8,32]{1,2,0,3:T(8,128)(2,1)}), bf16[2,192,8,32]{1,2,0,3:T(8,128)(2,1)S(1)}, u32[]{:S(2)}, u32[]{:S(2)}) async-start(bf16[2,192,8,32]{1,2,0,3:T(8,128)(2,1)} %copy.230), calls=%async_computation.1 | async-start | bytes 524288 | tf_op jit(solution)/shard_map/all_to_all | solution.py:33
  45.5 24.7 %copy-start.1 = (bf16[2,24,384]{2,1,0:T(8,128)(2,1)S(1)}, bf16[2,24,384]{2,1,0:T(8,128)(2,1)}, u32[]{:S(2)}) copy-start(bf16[2,24,384]{2,1,0:T(8,128)(2,1)} %param.21) | copy-start | bytes 110596
  45.5 14.8 %all-to-all-start.2 = ((bf16[64,192,8,1]{1,2,3,0:T(8,128)(2,1)}), bf16[64,192,8,1]{1,2,3,0:T(8,128)(2,1)S(1)}, u32[]{:S(2)}, u32[]{:S(2)}) async-start(bf16[64,192,8,1]{1,2,3,0:T(8,128)(2,1)} %copy.241), calls=%async_computation.2 | async-start | bytes 524288 | tf_op jit(solution)/shard_map/all_to_all | solution.py:33
  60.7 19.1 %copy-start.3 = (bf16[2,384]{1,0:T(2,128)(2,1)S(1)}, bf16[2,384]{1,0:T(2,128)(2,1)}, u32[]{:S(2)}) copy-start(bf16[2,384]{1,0:T(2,128)(2,1)} %param.22) | copy-start | bytes 4612
  60.8 19.1 %copy-start.5 = (f32[2,96]{1,0:T(2,128)S(1)}, f32[2,96]{1,0:T(2,128)}, u32[]{:S(2)}) copy-start(f32[2,96]{1,0:T(2,128)} %param.20) | copy-start | bytes 2308
  60.8 19.1 %copy-start.2 = (bf16[2,384,24]{1,2,0:T(8,128)(2,1)S(1)}, bf16[2,384,24]{1,2,0:T(8,128)(2,1)}, u32[]{:S(2)}) copy-start(bf16[2,384,24]{1,2,0:T(8,128)(2,1)} %param.23) | copy-start | bytes 110596
  62.3 12.7 %all-to-all-start.3 = ((f32[8,1,2048]{2,1,0:T(1,128)}), f32[8,1,2048]{2,1,0:T(1,128)S(1)}, u32[]{:S(2)}, u32[]{:S(2)}) async-start(f32[8,1,2048]{2,1,0:T(1,128)} %broadcast_in_dim.97), calls=%async_computation.3 | async-start | bytes 131072 | tf_op jit(solution)/shard_map/all_to_all | solution.py:14
  75.9 21.5 %all-to-all-start.4 = ((bf16[32,24,384]{2,1,0:T(8,128)(2,1)}), bf16[32,24,384]{2,1,0:T(8,128)(2,1)S(1)}, u32[]{:S(2)}, u32[]{:S(2)}) async-start(bf16[32,24,384]{2,1,0:T(8,128)(2,1)} %broadcast_in_dim.98), calls=%async_computation.4 | async-start | bytes 1179648 | tf_op jit(solution)/shard_map/all_to_all | solution.py:14
  98.3 35.2 %all-to-all-start.5 = ((bf16[32,384,24]{1,2,0:T(8,128)(2,1)}), bf16[32,384,24]{1,2,0:T(8,128)(2,1)S(1)}, u32[]{:S(2)}, u32[]{:S(2)}) async-start(bf16[32,384,24]{1,2,0:T(8,128)(2,1)} %broadcast_in_dim.99), calls=%async_computation.5 | async-start | bytes 1179648 | tf_op jit(solution)/shard_map/all_to_all | solution.py:14
  136.7 27.7 %all-to-all-start.6 = ((bf16[8,1024,96]{1,2,0:T(8,128)(2,1)}), bf16[8,1024,96]{1,2,0:T(8,128)(2,1)S(1)}, u32[]{:S(2)}, u32[]{:S(2)}) async-start(bf16[8,1024,96]{1,2,0:T(8,128)(2,1)} %bitcast.279), calls=%async_computation.6 | async-start | bytes 3145728 | tf_op jit(solution)/shard_map/all_to_all | solution.py:81
  165.5 9.1 %all-to-all-start.7 = ((f32[8,1,2048]{2,1,0:T(1,128)}), f32[8,1,2048]{2,1,0:T(1,128)S(1)}, u32[]{:S(2)}, u32[]{:S(2)}) async-start(f32[8,1,2048]{2,1,0:T(1,128)} %broadcast_in_dim.100), calls=%async_computation.7 | async-start | bytes 131072 | tf_op jit(solution)/shard_map/all_to_all | solution.py:14
  176.9 20.7 %all-to-all-start.8 = ((bf16[2,192,8,32]{1,2,0,3:T(8,128)(2,1)}), bf16[2,192,8,32]{1,2,0,3:T(8,128)(2,1)S(1)}, u32[]{:S(2)}, u32[]{:S(2)}) async-start(bf16[2,192,8,32]{1,2,0,3:T(8,128)(2,1)} %copy.251), calls=%async_computation.8 | async-start | bytes 524288 | tf_op jit(solution)/shard_map/all_to_all | solution.py:33
  230.3 21.5 %all-to-all-start.11 = ((bf16[32,24,384]{2,1,0:T(8,128)(2,1)}), bf16[32,24,384]{2,1,0:T(8,128)(2,1)S(1)}, u32[]{:S(2)}, u32[]{:S(2)}) async-start(bf16[32,24,384]{2,1,0:T(8,128)(2,1)} %broadcast_in_dim.102), calls=%async_computation.11 | async-start | bytes 1179648 | tf_op jit(solution)/shard_map/all_to_all | solution.py:14
  252.7 35.4 %all-to-all-start.12 = ((bf16[32,384,24]{1,2,0:T(8,128)(2,1)}), bf16[32,384,24]{1,2,0:T(8,128)(2,1)}, u32[]{:S(2)}, u32[]{:S(2)}) async-start(bf16[32,384,24]{1,2,0:T(8,128)(2,1)} %broadcast_in_dim.103), calls=%async_computation.12 | async-start | bytes 1179648 | tf_op jit(solution)/shard_map/all_to_all | solution.py:14
where the time goes:
time: 322 us; the launch traced here: 321 us
  blocking collectives  113 us (35%)
  waiting for transfers between devices  96 us (30%)
  starting transfers between devices  68.2 us (21%)
  matrix products  18.4 us (6%)
  local copies, waits for them, and re-layouts  17.4 us (5%)
  other arithmetic  7.38 us (2%)
    all_gather x8, blocking collectives, stacked_from(): tiles = lax.all_gather(tiles, axes[k], axis=0, tiled=True)  59.3 us
    all_to_all x7, waiting for transfers between devices, from_everyone(): return lax.all_to_all(copies, axis, split_axis=0, concat_axis=0, tiled=True)  43.9 us
    all_to_all x7, starting transfers between devices, from_everyone(): return lax.all_to_all(copies, axis, split_axis=0, concat_axis=0, tiled=True)  36.8 us
    all_to_all x3, waiting for transfers between devices, sent_together(): lax.all_to_all(both, axis, split_axis=split_dim, concat_axis=concat_dim,...  32 us
    all_to_all x1, blocking collectives, summed_on_arrival(): lax.all_to_all(tiles, axis, split_axis=0, concat_axis=0, tiled=True)  27.6 us
    all_to_all x3, starting transfers between devices, sent_together(): lax.all_to_all(both, axis, split_axis=split_dim, concat_axis=concat_dim,...  24.3 us
    all_to_all x1, waiting for transfers between devices, summed_on_arrival(): lax.all_to_all(tiles, axis, split_axis=0, concat_axis=0, tiled=True)  20.1 us
    all_to_all x1, blocking collectives, sent_together(): lax.all_to_all(both, axis, split_axis=split_dim, concat_axis=concat_dim,...  14.9 us
  transfers between devices with their start and end apart: 11, of which 8 were waited for; matrix products, arithmetic and copies ran while one was open for 3% of the time, Pallas kernels for 0%

commit v1 on v0

--- a/solution.py
+++ b/solution.py
@@ -42,7 +42,10 @@
 def stacked_from(value, axes, sequence):
     tiles = value[None]
     for k in sequence:
-        tiles = lax.all_gather(tiles, axes[k], axis=0, tiled=True)
+        my_data = axes[k]
+        tiles = jnp.concatenate(
+            lax.all_to_all(jnp.stack([tiles] * lax.psum(1, my_data), axis=0), my_data, 0, 0), axis=0
+        )
     held = [lax.axis_size(axes[k]) for k in reversed(sequence)]
     tiles = tiles.reshape(*held, *value.shape)
     turned = sorted(range(len(sequence)), key=lambda place: sequence[len(sequence) - 1 - place])

time: 322 us -> 368 us (1.14)
  waiting for transfers between devices: 96 us -> 147 us
  blocking collectives: 113 us -> 88.7 us
  starting transfers between devices: 68.2 us -> 76 us
  local copies, waits for them, and re-layouts: 17.4 us -> 22.1 us
  other arithmetic: 7.38 us -> 11.2 us
    all_gather x8 -> x0, blocking collectives: 59.3 us -> none  [stacked_from(): tiles = lax.all_gather(tiles, axes[k], axis=0, tiled=True)]
    all_to_all x1 -> x6, blocking collectives: 11 us -> 46.5 us  [stacked_from(): lax.all_to_all(jnp.stack([tiles] * lax.psum(1, my_data), axis=0), my_data...]
    all_to_all x7 -> x8, waiting for transfers between devices: 43.9 us -> 76.3 us  [from_everyone(): return lax.all_to_all(copies, axis, split_axis=0, concat_axis=0, tiled=True)]
    all_to_all x0 -> x2, waiting for transfers between devices: none -> 18.5 us  [stacked_from(): lax.all_to_all(jnp.stack([tiles] * lax.psum(1, my_data), axis=0), my_data...]
    all_to_all x0 -> x2, starting transfers between devices: none -> 7.08 us  [stacked_from(): lax.all_to_all(jnp.stack([tiles] * lax.psum(1, my_data), axis=0), my_data...]
    all_to_all x7 -> x8, starting transfers between devices: 36.8 us -> 42.7 us  [from_everyone(): return lax.all_to_all(copies, axis, split_axis=0, concat_axis=0, tiled=True)]
    all_to_all x3, starting transfers between devices: 24.3 us -> 19.4 us  [sent_together(): lax.all_to_all(both, axis, split_axis=split_dim, concat_axis=concat_dim,...]
  transfers between devices with their start and end apart: 11 -> 14, of which waited for: 8 -> 13; matrix products, arithmetic and copies ran while one was open for 3% -> 4% of each run, Pallas kernels for 0% -> 0%
where the time goes in v1:
time: 368 us; the launch traced here: 366 us
  waiting for transfers between devices  147 us (40%)
  blocking collectives  88.7 us (24%)
  starting transfers between devices  76 us (21%)
  local copies, waits for them, and re-layouts  22.1 us (6%)
  matrix products  20.2 us (5%)
  other arithmetic  11.2 us (3%)
    all_to_all x8, waiting for transfers between devices, from_everyone(): return lax.all_to_all(copies, axis, split_axis=0, concat_axis=0, tiled=True)  76.3 us
    all_to_all x6, blocking collectives, stacked_from(): lax.all_to_all(jnp.stack([tiles] * lax.psum(1, my_data), axis=0), my_data...  46.5 us
    all_to_all x8, starting transfers between devices, from_everyone(): return lax.all_to_all(copies, axis, split_axis=0, concat_axis=0, tiled=True)  42.7 us
    all_to_all x3, waiting for transfers between devices, sent_together(): lax.all_to_all(both, axis, split_axis=split_dim, concat_axis=concat_dim,...  32 us
    all_to_all x1, blocking collectives, summed_on_arrival(): lax.all_to_all(tiles, axis, split_axis=0, concat_axis=0, tiled=True)  27.3 us
    all_to_all x1, waiting for transfers between devices, summed_on_arrival(): lax.all_to_all(tiles, axis, split_axis=0, concat_axis=0, tiled=True)  20.1 us
    all_to_all x3, starting transfers between devices, sent_together(): lax.all_to_all(both, axis, split_axis=split_dim, concat_axis=concat_dim,...  19.4 us
    all_to_all x2, waiting for transfers between devices, stacked_from(): lax.all_to_all(jnp.stack([tiles] * lax.psum(1, my_data), axis=0), my_data...  18.5 us
  transfers between devices with their start and end apart: 14, of which 13 were waited for; matrix products, arithmetic and copies ran while one was open for 4% of the time, Pallas kernels for 0%

profile of v1, /device:TPU:1, one launch (start us, length us, event | category | flops | bytes accessed | tf_op | source)
XLA Modules:
  0.0 366.2 jit_solution(11581247689867492733)
XLA Ops:
  1.8 6.5 %all-to-all-start = ((f32[8,1,2048]{2,1,0:T(1,128)}), f32[8,1,2048]{2,1,0:T(1,128)S(1)}, u32[]{:S(2)}, u32[]{:S(2)}) async-start(f32[8,1,2048]{2,1,0:T(1,128)} %broadcast_in_dim.88), calls=%async_computation | async-start | bytes 131072 | tf_op jit(solution)/shard_map/all_to_all | solution.py:14
  18.9 10.6 %all-to-all-start.1 = ((bf16[2,192,8,32]{1,2,0,3:T(8,128)(2,1)}), bf16[2,192,8,32]{1,2,0,3:T(8,128)(2,1)S(1)}, u32[]{:S(2)}, u32[]{:S(2)}) async-start(bf16[2,192,8,32]{1,2,0,3:T(8,128)(2,1)} %copy.228), calls=%async_computation.1 | async-start | bytes 524288 | tf_op jit(solution)/shard_map/all_to_all | solution.py:33
  30.1 11.2 %all-to-all-done.1 = bf16[2,192,8,32]{1,2,0,3:T(8,128)(2,1)S(1)} async-done(((bf16[2,192,8,32]{1,2,0,3:T(8,128)(2,1)}), bf16[2,192,8,32]{1,2,0,3:T(8,128)(2,1)S(1)}, u32[]{:S(2)}, u32[]{:S(2)}) %all-to-all-start.1) | async-done | bytes 196640 | tf_op jit(solution)/shard_map/all_to_all | solution.py:33
  51.2 10.2 %all-to-all-done.2 = bf16[64,192,8,1]{1,2,3,0:T(8,128)(2,1)S(1)} async-done(((bf16[64,192,8,1]{1,2,3,0:T(8,128)(2,1)}), bf16[64,192,8,1]{1,2,3,0:T(8,128)(2,1)S(1)}, u32[]{:S(2)}, u32[]{:S(2)}) %all-to-all-start.2) | async-done | bytes 196640 | tf_op jit(solution)/shard_map/all_to_all | solution.py:33
  63.5 7.8 %all-to-all-start.3 = ((f32[8,1,2048]{2,1,0:T(1,128)}), f32[8,1,2048]{2,1,0:T(1,128)S(1)}, u32[]{:S(2)}, u32[]{:S(2)}) async-start(f32[8,1,2048]{2,1,0:T(1,128)} %broadcast_in_dim.93), calls=%async_computation.3 | async-start | bytes 131072 | tf_op jit(solution)/shard_map/all_to_all | solution.py:14
  85.6 7.2 %all-to-all-done.4 = bf16[4,1,512,96]{2,3,1,0:T(8,128)(2,1)S(1)} async-done(((bf16[4,1,512,96]{2,3,1,0:T(8,128)(2,1)}), bf16[4,1,512,96]{2,3,1,0:T(8,128)(2,1)S(1)}, u32[]{:S(2)}, u32[]{:S(2)}) %all-to-all-start.4) | async-done | bytes 393248 | tf_op jit(solution)/shard_map/all_to_all | solution.py:47
  97.6 17.1 %all-to-all-done.8 = bf16[32,24,384]{2,1,0:T(8,128)(2,1)S(1)} async-done(((bf16[32,24,384]{2,1,0:T(8,128)(2,1)}), bf16[32,24,384]{2,1,0:T(8,128)(2,1)S(1)}, u32[]{:S(2)}, u32[]{:S(2)}) %all-to-all-start.8) | async-done | bytes 589856 | tf_op jit(solution)/shard_map/all_to_all | solution.py:14
  114.7 6.7 %all_to_all.167 = bf16[2,4,512,96]{2,3,1,0:T(8,128)(2,1)S(1)} all-to-all(bf16[2,4,512,96]{2,3,1,0:T(8,128)(2,1)S(1)} %pad_maximum_fusion.2), channel_id=1, replica_groups=mesh['rows'=32,'chan_0'=4,'chan_1'=2] {'chan_1'}, dimensions={0} | all-to-all | bytes 1572864 | tf_op jit(solution)/shard_map/all_to_all | solution.py:47
  126.6 11.4 %all-to-all-done.7 = bf16[4,2,512,96]{2,3,1,0:T(8,128)(2,1)S(1)} async-done(((bf16[4,2,512,96]{2,3,1,0:T(8,128)(2,1)}), bf16[4,2,512,96]{2,3,1,0:T(8,128)(2,1)S(1)}, u32[]{:S(2)}, u32[]{:S(2)}) %all-to-all-start.7) | async-done | bytes 786464 | tf_op jit(solution)/shard_map/all_to_all | solution.py:47
  138.8 4.8 %all-to-all-start.9 = ((bf16[32,384,24]{1,2,0:T(8,128)(2,1)}), bf16[32,384,24]{1,2,0:T(8,128)(2,1)S(1)}, u32[]{:S(2)}, u32[]{:S(2)}) async-start(bf16[32,384,24]{1,2,0:T(8,128)(2,1)} %broadcast_in_dim.95), calls=%async_computation.9 | async-start | bytes 1179648 | tf_op jit(solution)/shard_map/all_to_all | solution.py:14
  145.7 14.4 %all-to-all-done.9 = bf16[32,384,24]{1,2,0:T(8,128)(2,1)S(1)} async-done(((bf16[32,384,24]{1,2,0:T(8,128)(2,1)}), bf16[32,384,24]{1,2,0:T(8,128)(2,1)S(1)}, u32[]{:S(2)}, u32[]{:S(2)}) %all-to-all-start.9) | async-done | bytes 589856 | tf_op jit(solution)/shard_map/all_to_all | solution.py:14
  164.7 6.7 %all-to-all-start.10 = ((bf16[8,1024,96]{1,2,0:T(8,128)(2,1)}), bf16[8,1024,96]{1,2,0:T(8,128)(2,1)S(1)}, u32[]{:S(2)}, u32[]{:S(2)}) async-start(bf16[8,1024,96]{1,2,0:T(8,128)(2,1)} %bitcast.291), calls=%async_computation.10 | async-start | bytes 3145728 | tf_op jit(solution)/shard_map/all_to_all | solution.py:84
  172.0 20.1 %all-to-all-done.10 = bf16[8,1024,96]{1,2,0:T(8,128)(2,1)S(1)} async-done(((bf16[8,1024,96]{1,2,0:T(8,128)(2,1)}), bf16[8,1024,96]{1,2,0:T(8,128)(2,1)S(1)}, u32[]{:S(2)}, u32[]{:S(2)}) %all-to-all-start.10) | async-done | bytes 1572896 | tf_op jit(solution)/shard_map/all_to_all | solution.py:84
  209.8 10.5 %all-to-all-done.12 = bf16[2,192,8,32]{1,2,0,3:T(8,128)(2,1)S(1)} async-done(((bf16[2,192,8,32]{1,2,0,3:T(8,128)(2,1)}), bf16[2,192,8,32]{1,2,0,3:T(8,128)(2,1)S(1)}, u32[]{:S(2)}, u32[]{:S(2)}) %all-to-all-start.12) | async-done | bytes 196640 | tf_op jit(solution)/shard_map/all_to_all | solution.py:33
  225.0 14.9 %all_to_all.168 = bf16[64,192,8,1]{1,2,3,0:T(8,128)(2,1)S(1)} all-to-all(bf16[64,192,8,1]{1,2,3,0:T(8,128)(2,1)S(1)} %copy.260), channel_id=1, replica_groups=mesh['rows'=32,'chan_0'=4,'chan_1'=2] {'rows'}, dimensions={0} | all-to-all | bytes 393216 | tf_op jit(solution)/shard_map/all_to_all | solution.py:33
  241.9 7.0 %all-to-all-start.14 = ((f32[8,1,2048]{2,1,0:T(1,128)}), f32[8,1,2048]{2,1,0:T(1,128)S(1)}, u32[]{:S(2)}, u32[]{:S(2)}) async-start(f32[8,1,2048]{2,1,0:T(1,128)} %broadcast_in_dim.97), calls=%async_computation.14 | async-start | bytes 131072 | tf_op jit(solution)/shard_map/all_to_all | solution.py:14
  249.1 4.7 %all-to-all-done.14 = f32[8,1,2048]{2,1,0:T(1,128)S(1)} async-done(((f32[8,1,2048]{2,1,0:T(1,128)}), f32[8,1,2048]{2,1,0:T(1,128)S(1)}, u32[]{:S(2)}, u32[]{:S(2)}) %all-to-all-start.14) | async-done | bytes 65568 | tf_op jit(solution)/shard_map/all_to_all | solution.py:14
  254.0 9.5 %all_to_all.169 = bf16[4,1,512,96]{2,3,1,0:T(8,128)(2,1)S(1)} all-to-all(bf16[4,1,512,96]{2,3,1,0:T(8,128)(2,1)S(1)} %stack.28), channel_id=1, replica_groups=mesh['rows'=32,'chan_0'=4,'chan_1'=2] {'chan_0'}, dimensions={0} | all-to-all | bytes 786432 | tf_op jit(solution)/shard_map/all_to_all | solution.py:47
  268.4 16.4 %all-to-all-done.19 = bf16[32,24,384]{2,1,0:T(8,128)(2,1)S(1)} async-done(((bf16[32,24,384]{2,1,0:T(8,128)(2,1)}), bf16[32,24,384]{2,1,0:T(8,128)(2,1)S(1)}, u32[]{:S(2)}, u32[]{:S(2)}) %all-to-all-start.19) | async-done | bytes 589856 | tf_op jit(solution)/shard_map/all_to_all | solution.py:14
  284.8 7.0 %all_to_all.170 = bf16[2,1,512,96]{2,3,1,0:T(8,128)(2,1)S(1)} all-to-all(bf16[2,1,512,96]{2,3,1,0:T(8,128)(2,1)S(1)} %pad_maximum_fusion.11), channel_id=1, replica_groups=mesh['rows'=32,'chan_0'=4,'chan_1'=2] {'chan_1'}, dimensions={0} | all-to-all | bytes 393216 | tf_op jit(solution)/shard_map/all_to_all | solution.py:47
  296.3 14.6 %all_to_all.172 = bf16[4,2,512,96]{2,3,1,0:T(8,128)(2,1)S(1)} all-to-all(bf16[4,2,512,96]{2,3,1,0:T(8,128)(2,1)S(1)} %stack.31), channel_id=1, replica_groups=mesh['rows'=32,'chan_0'=4,'chan_1'=2] {'chan_0'}, dimensions={0} | all-to-all | bytes 1572864 | tf_op jit(solution)/shard_map/all_to_all | solution.py:47
  317.9 15.2 %all-to-all-done.20 = bf16[32,384,24]{1,2,0:T(8,128)(2,1)} async-done(((bf16[32,384,24]{1,2,0:T(8,128)(2,1)}), bf16[32,384,24]{1,2,0:T(8,128)(2,1)}, u32[]{:S(2)}, u32[]{:S(2)}) %all-to-all-start.20) | async-done | bytes 589856 | tf_op jit(solution)/shard_map/all_to_all | solution.py:14
  333.1 4.7 %convolution_convert_fusion = bf16[1024,768]{0,1:T(8,128)(2,1)} fusion(bf16[384,768]{0,1:T(8,128)(2,1)} %bitcast.112, bf16[1024,768]{0,1:T(8,128)(2,1)} %bitcast.292, bf16[768,384]{1,0:T(8,128)(2,1)S(1)} %bitcast.314, f32[384]{0:T(512)S(1)} %copy-done.9), kind=kOutput, calls=%fused_computation.4 | convolution fusion | flops 1212678144 | bytes 4326912 | tf_op jit(solution)/shard_map/dot_general | solution.py:205
  337.7 27.3 %all_to_all.173 = bf16[8,1024,96]{1,2,0:T(8,128)(2,1)S(1)} all-to-all(bf16[8,1024,96]{1,2,0:T(8,128)(2,1)} %bitcast.294), channel_id=1, replica_groups=mesh['rows'=32,'chan_0'=4,'chan_1'=2] {'chan_0','chan_1'}, dimensions={0} | all-to-all | bytes 3145728 | tf_op jit(solution)/shard_map/all_to_all | solution.py:84
  (214 shorter events, 98.6 us)
Async XLA Ops:
  1.8 14.8 %all-to-all-start = ((f32[8,1,2048]{2,1,0:T(1,128)}), f32[8,1,2048]{2,1,0:T(1,128)S(1)}, u32[]{:S(2)}, u32[]{:S(2)}) async-start(f32[8,1,2048]{2,1,0:T(1,128)} %broadcast_in_dim.88), calls=%async_computation | async-start | bytes 131072 | tf_op jit(solution)/shard_map/all_to_all | solution.py:14
  18.9 22.5 %all-to-all-start.1 = ((bf16[2,192,8,32]{1,2,0,3:T(8,128)(2,1)}), bf16[2,192,8,32]{1,2,0,3:T(8,128)(2,1)S(1)}, u32[]{:S(2)}, u32[]{:S(2)}) async-start(bf16[2,192,8,32]{1,2,0,3:T(8,128)(2,1)} %copy.228), calls=%async_computation.1 | async-start | bytes 524288 | tf_op jit(solution)/shard_map/all_to_all | solution.py:33
  46.7 24.6 %copy-start.13 = (f32[2,96]{1,0:T(2,128)S(1)}, f32[2,96]{1,0:T(2,128)}, u32[]{:S(2)}) copy-start(f32[2,96]{1,0:T(2,128)} %param.20) | copy-start | bytes 2308
  46.7 14.8 %all-to-all-start.2 = ((bf16[64,192,8,1]{1,2,3,0:T(8,128)(2,1)}), bf16[64,192,8,1]{1,2,3,0:T(8,128)(2,1)S(1)}, u32[]{:S(2)}, u32[]{:S(2)}) async-start(bf16[64,192,8,1]{1,2,3,0:T(8,128)(2,1)} %copy.239), calls=%async_computation.2 | async-start | bytes 524288 | tf_op jit(solution)/shard_map/all_to_all | solution.py:33
  63.5 12.7 %all-to-all-start.3 = ((f32[8,1,2048]{2,1,0:T(1,128)}), f32[8,1,2048]{2,1,0:T(1,128)S(1)}, u32[]{:S(2)}, u32[]{:S(2)}) async-start(f32[8,1,2048]{2,1,0:T(1,128)} %broadcast_in_dim.93), calls=%async_computation.3 | async-start | bytes 131072 | tf_op jit(solution)/shard_map/all_to_all | solution.py:14
  72.0 12.9 %copy-start.6 = (bf16[2,24,384]{2,1,0:T(8,128)(2,1)S(1)}, bf16[2,24,384]{2,1,0:T(8,128)(2,1)}, u32[]{:S(2)}) copy-start(bf16[2,24,384]{2,1,0:T(8,128)(2,1)} %param.21) | copy-start | bytes 110596
  81.5 11.2 %all-to-all-start.4 = ((bf16[4,1,512,96]{2,3,1,0:T(8,128)(2,1)}), bf16[4,1,512,96]{2,3,1,0:T(8,128)(2,1)S(1)}, u32[]{:S(2)}, u32[]{:S(2)}) async-start(bf16[4,1,512,96]{2,3,1,0:T(8,128)(2,1)} %stack.24), calls=%async_computation.4 | async-start | bytes 786432 | tf_op jit(solution)/shard_map/all_to_all | solution.py:47
  93.6 21.0 %all-to-all-start.8 = ((bf16[32,24,384]{2,1,0:T(8,128)(2,1)}), bf16[32,24,384]{2,1,0:T(8,128)(2,1)S(1)}, u32[]{:S(2)}, u32[]{:S(2)}) async-start(bf16[32,24,384]{2,1,0:T(8,128)(2,1)} %broadcast_in_dim.94), calls=%async_computation.8 | async-start | bytes 1179648 | tf_op jit(solution)/shard_map/all_to_all | solution.py:14
  122.3 21.3 %copy-start.8 = (bf16[2,384]{1,0:T(2,128)(2,1)S(1)}, bf16[2,384]{1,0:T(2,128)(2,1)}, u32[]{:S(2)}) copy-start(bf16[2,384]{1,0:T(2,128)(2,1)} %param.22) | copy-start | bytes 4612
  122.3 15.6 %all-to-all-start.7 = ((bf16[4,2,512,96]{2,3,1,0:T(8,128)(2,1)}), bf16[4,2,512,96]{2,3,1,0:T(8,128)(2,1)S(1)}, u32[]{:S(2)}, u32[]{:S(2)}) async-start(bf16[4,2,512,96]{2,3,1,0:T(8,128)(2,1)} %stack.27), calls=%async_computation.7 | async-start | bytes 1572864 | tf_op jit(solution)/shard_map/all_to_all | solution.py:47
  138.8 21.3 %all-to-all-start.9 = ((bf16[32,384,24]{1,2,0:T(8,128)(2,1)}), bf16[32,384,24]{1,2,0:T(8,128)(2,1)S(1)}, u32[]{:S(2)}, u32[]{:S(2)}) async-start(bf16[32,384,24]{1,2,0:T(8,128)(2,1)} %broadcast_in_dim.95), calls=%async_computation.9 | async-start | bytes 1179648 | tf_op jit(solution)/shard_map/all_to_all | solution.py:14
  164.7 27.4 %all-to-all-start.10 = ((bf16[8,1024,96]{1,2,0:T(8,128)(2,1)}), bf16[8,1024,96]{1,2,0:T(8,128)(2,1)S(1)}, u32[]{:S(2)}, u32[]{:S(2)}) async-start(bf16[8,1024,96]{1,2,0:T(8,128)(2,1)} %bitcast.291), calls=%async_computation.10 | async-start | bytes 3145728 | tf_op jit(solution)/shard_map/all_to_all | solution.py:84
  172.0 25.4 %copy-start.1 = (f32[1,96,128]{2,1,0:T(8,128)S(1)}, f32[1,96,128]{2,1,0:T(8,128)}, u32[]{:S(2)}) copy-start(f32[1,96,128]{2,1,0:T(8,128)} %get-tuple-element.75) | copy-start | bytes 147460
  192.3 10.0 %copy-start.10 = (f32[96]{0:T(128)S(1)}, f32[96]{0:T(128)}, u32[]{:S(2)}) copy-start(f32[96]{0:T(128)} %get-tuple-element.140) | copy-start | bytes 1156
  193.2 9.1 %all-to-all-start.11 = ((f32[8,1,2048]{2,1,0:T(1,128)}), f32[8,1,2048]{2,1,0:T(1,128)S(1)}, u32[]{:S(2)}, u32[]{:S(2)}) async-start(f32[8,1,2048]{2,1,0:T(1,128)} %broadcast_in_dim.96), calls=%async_computation.11 | async-start | bytes 131072 | tf_op jit(solution)/shard_map/all_to_all | solution.py:14
  197.4 5.7 %copy-start.3 = (f32[64,32]{0,1:T(8,128)S(1)}, f32[64,32]{0,1:T(8,128)}, u32[]{:S(2)}) copy-start(f32[64,32]{0,1:T(8,128)} %copy-done.2) | copy-start | bytes 24580
  204.6 15.8 %all-to-all-start.12 = ((bf16[2,192,8,32]{1,2,0,3:T(8,128)(2,1)}), bf16[2,192,8,32]{1,2,0,3:T(8,128)(2,1)S(1)}, u32[]{:S(2)}, u32[]{:S(2)}) async-start(bf16[2,192,8,32]{1,2,0,3:T(8,128)(2,1)} %copy.249), calls=%async_computation.12 | async-start | bytes 524288 | tf_op jit(solution)/shard_map/all_to_all | solution.py:33
  240.0 13.9 %copy-start.11 = (f32[96]{0:T(128)S(1)}, f32[96]{0:T(128)}, u32[]{:S(2)}) copy-start(f32[96]{0:T(128)} %get-tuple-element.138) | copy-start | bytes 1156
  241.9 11.9 %all-to-all-start.14 = ((f32[8,1,2048]{2,1,0:T(1,128)}), f32[8,1,2048]{2,1,0:T(1,128)S(1)}, u32[]{:S(2)}, u32[]{:S(2)}) async-start(f32[8,1,2048]{2,1,0:T(1,128)} %broadcast_in_dim.97), calls=%async_computation.14 | async-start | bytes 131072 | tf_op jit(solution)/shard_map/all_to_all | solution.py:14
  248.9 14.6 %copy-start.4 = (bf16[24,384]{1,0:T(8,128)(2,1)S(1)}, bf16[24,384]{1,0:T(8,128)(2,1)}, u32[]{:S(2)}) copy-start(bf16[24,384]{1,0:T(8,128)(2,1)} %get-tuple-element.126) | copy-start | bytes 55300
  264.4 20.4 %all-to-all-start.19 = ((bf16[32,24,384]{2,1,0:T(8,128)(2,1)}), bf16[32,24,384]{2,1,0:T(8,128)(2,1)S(1)}, u32[]{:S(2)}, u32[]{:S(2)}) async-start(bf16[32,24,384]{2,1,0:T(8,128)(2,1)} %broadcast_in_dim.98), calls=%async_computation.19 | async-start | bytes 1179648 | tf_op jit(solution)/shard_map/all_to_all | solution.py:14
  296.2 14.7 %copy-start.5 = (bf16[384,24]{0,1:T(8,128)(2,1)S(1)}, bf16[384,24]{0,1:T(8,128)(2,1)}, u32[]{:S(2)}) copy-start(bf16[384,24]{0,1:T(8,128)(2,1)} %get-tuple-element.128) | copy-start | bytes 55300
  311.8 21.3 %all-to-all-start.20 = ((bf16[32,384,24]{1,2,0:T(8,128)(2,1)}), bf16[32,384,24]{1,2,0:T(8,128)(2,1)}, u32[]{:S(2)}, u32[]{:S(2)}) async-start(bf16[32,384,24]{1,2,0:T(8,128)(2,1)} %broadcast_in_dim.99), calls=%async_computation.20 | async-start | bytes 1179648 | tf_op jit(solution)/shard_map/all_to_all | solution.py:14
  316.5 16.6 %copy-start.9 = (f32[384]{0:T(512)S(1)}, f32[384]{0:T(512)}, u32[]{:S(2)}) copy-start(f32[384]{0:T(512)} %get-tuple-element.65) | copy-start | bytes 4612
  (4 other events, 14.0 us)
